TPU v7x, 32 devices: a whole 2x2x4 slice. The times are simulated.
32 devices in a mesh: task: 2 (over x), batch: 16 (over z, y, core).
Axes of the slice: x: 2, y: 2, z: 4, core: 2. Of those that a mesh axis runs over, the one named last changes fastest.
Arguments:
- pooled: bfloat16 [12288, 3328], P('batch'), may hold values from -6 to 6
- gate_weight: bfloat16 [3328, 8, 4], P(None, 'task'), may hold values from -0.21875 to 0.21875
- w_first: bfloat16 [8, 3328, 1024], P('task', 'batch'), may hold values from -0.15625 to 0.15625
- w_second: bfloat16 [8, 1024, 512], P('task', 'batch'), may hold values from -0.25 to 0.25
- w_third: bfloat16 [8, 512, 256], P('task', 'batch'), may hold values from -0.375 to 0.375
- tower_hidden: bfloat16 [4, 256, 128], P('task'), may hold values from -0.5 to 0.5
- tower_out: bfloat16 [4, 128], P('task'), may hold values from -0.75 to 0.75
Outputs:
- task_logits: float32 [12288, 4], P('batch', 'task')
All inputs are finite; a program needn't handle non-finite values.
Results may differ from a plain program's by a relative error of at most 0.02.
Values may be sent and summed in bfloat16 or wider, within the bound.
A program may use at most 128 MiB of HBM per device.

v0:
```python
import functools

import jax
import jax.numpy as jnp
from jax import lax
from jax.experimental import pallas as pl
from jax.experimental.pallas import tpu as pltpu
from jax.sharding import PartitionSpec as P

MESH = pl.DeviceIdType.MESH
BF16, F32 = jnp.bfloat16, jnp.float32
VMEM_BYTES = 63 * 1024 * 1024


def dot(a, b):
    return jnp.dot(a, b, preferred_element_type=F32)


def fused_kernel(
    nb, tiles, deep_rows,
    pooled, gate, w_first, w_second, w_third, tower_hidden, tower_out, out,
    buf, dbuf, first, outs, outs_rx, wts, wts_rx, acc,
    loc, recv, szp, szm, sy, ssib, brecv, bzp, bzm, by, bsib, xs, xr, ws, wr,
):
    t, b = lax.axis_index("task"), lax.axis_index("batch")
    nz = nb // 4
    z, y, c = b // 4, (b // 2) % 2, b % 2
    experts = outs.shape[0]
    tasks = tower_hidden.shape[0]
    chunks = buf.shape[0]
    wide = buf.shape[3]
    tile = pooled.shape[0] // tiles

    def at(zz, yy, cc):
        return zz * 4 + yy * 2 + cc

    across, sib = at(z, 1 - y, c), at(z, y, 1 - c)
    up, down = at(z + 1, y, c), at(z - 1, y, c)

    def own_copy(k):
        return pltpu.make_async_copy(
            w_first.at[k // 2, :, pl.ds(pl.multiple_of((k % 2) * wide, 128), wide)],
            buf.at[k, b], loc.at[k],
        )

    pieces = w_second.shape[2] // w_third.shape[2]
    deep_copies = [
        pltpu.make_async_copy(
            w_second.at[:, :, pl.ds(h * w_third.shape[2], w_third.shape[2])],
            dbuf.at[b, :, pl.ds(h * deep_rows, deep_rows)], loc.at[chunks + h],
        )
        for h in range(pieces)
    ] + [
        pltpu.make_async_copy(
            w_third, dbuf.at[b, :, pl.ds(pieces * deep_rows, w_third.shape[1])],
            loc.at[chunks + pieces],
        )
    ]
    for copy in deep_copies:
        copy.start()

    @pl.loop(0, chunks)
    def _(k):
        own_copy(k).start()

    barrier = pltpu.get_barrier_semaphore()
    for peer in (across, sib, at((z + 1) % nz, y, c), at((z + nz - 1) % nz, y, c)):
        pl.semaphore_signal(barrier, inc=1, device_id=(t, peer), device_id_type=MESH)
    pl.semaphore_signal(barrier, inc=1, device_id=(1 - t, b), device_id_type=MESH)
    pl.semaphore_wait(barrier, 5)

    def move(k, slot, sem, dev):
        return pltpu.make_async_remote_copy(
            src_ref=buf.at[k, slot], dst_ref=buf.at[k, slot], send_sem=sem,
            recv_sem=recv.at[k, slot], device_id=(t, dev), device_id_type=MESH,
        )

    def bmove(slot, sem, dev):
        return pltpu.make_async_remote_copy(
            src_ref=dbuf.at[slot], dst_ref=dbuf.at[slot], send_sem=sem,
            recv_sem=brecv.at[slot], device_id=(t, dev), device_id_type=MESH,
        )

    def arrived(k, slot):
        move(k, slot, sy.at[0, 0], sib).wait_recv()

    def barrived(slot):
        bmove(slot, by.at[0], sib).wait_recv()

    def own_z(k):
        @pl.when(z < nz - 1)
        def _():
            move(k, b, szp.at[k, z], up).start()

        @pl.when(z > 0)
        def _():
            move(k, b, szm.at[k, z], down).start()

    def z_step(k, d):
        @pl.when(z >= d)
        def _():
            slot = at(z - d, y, c)
            arrived(k, slot)

            @pl.when(z < nz - 1)
            def _():
                move(k, slot, szp.at[k, z - d], up).start()

            move(k, slot, sy.at[k, z - d], across).start()
            move(k, slot, ssib.at[k, z - d], sib).start()

        @pl.when(z + d < nz)
        def _():
            slot = at(z + d, y, c)
            arrived(k, slot)

            @pl.when(z > 0)
            def _():
                move(k, slot, szm.at[k, z + d], down).start()

            move(k, slot, sy.at[k, z + d], across).start()
            move(k, slot, ssib.at[k, z + d], sib).start()

    def y_step(k):
        @pl.loop(0, nz)
        def _(zz):
            slot = at(zz, 1 - y, c)
            arrived(k, slot)
            move(k, slot, ssib.at[k, nz + zz], sib).start()

    def sib_wait(k):
        @pl.loop(0, nz * 2)
        def _(q):
            arrived(k, q * 2 + (1 - c))

    def b_send_z(slot, yy, zz):
        @pl.when(jnp.logical_and(z < nz - 1, zz <= z))
        def _():
            bmove(slot, bzp.at[yy, zz], up).start()

        @pl.when(jnp.logical_and(z > 0, zz >= z))
        def _():
            bmove(slot, bzm.at[yy, zz], down).start()

    for copy in deep_copies:
        copy.wait()
    bmove(b, by.at[0], across).start()
    b_send_z(b, y, z)
    bmove(b, bsib.at[y, z], sib).start()

    @pl.loop(0, chunks)
    def _(k):
        own_copy(k).wait()
        move(k, b, sy.at[k, z], across).start()
        move(k, b, ssib.at[k, z], sib).start()

    barrived(across)
    b_send_z(across, 1 - y, z)
    bmove(across, bsib.at[1 - y, z], sib).start()
    own_z(0)

    for m in range(tiles):
        rows = pl.ds(m * tile, tile)
        wts[rows, :] = jnp.exp(dot(pooled[rows, :], gate[...]))
    w_move = pltpu.make_async_remote_copy(
        src_ref=wts, dst_ref=wts_rx, send_sem=ws.at[0], recv_sem=wr.at[0],
        device_id=(1 - t, b), device_id_type=MESH,
    )
    w_move.start()
    acc[...] = jnp.zeros_like(acc)

    for d in range(1, nz):
        for same in (True, False):
            yy = y if same else 1 - y

            @pl.when(z >= d)
            def _():
                slot = at(z - d, yy, c)
                barrived(slot)
                b_send_z(slot, yy, z - d)
                bmove(slot, bsib.at[yy, z - d], sib).start()

            @pl.when(z + d < nz)
            def _():
                slot = at(z + d, yy, c)
                barrived(slot)
                b_send_z(slot, yy, z + d)
                bmove(slot, bsib.at[yy, z + d], sib).start()

    @pl.loop(0, nz * 2)
    def _(q):
        barrived(q * 2 + (1 - c))

    w_move.wait_recv()

    def x_move(e, m):
        rows = pl.ds(m * tile, tile)
        return pltpu.make_async_remote_copy(
            src_ref=outs.at[e, rows], dst_ref=outs_rx.at[e, rows],
            send_sem=xs.at[e, m], recv_sem=xr.at[e, m],
            device_id=(1 - t, b), device_id_type=MESH,
        )

    def accumulate(w_ref, base, e, m, value):
        rows = pl.ds(m * tile, tile)
        w = w_ref[rows, :]
        lane = lax.broadcasted_iota(jnp.int32, w.shape, 1)
        value = value.astype(F32)
        for j in range(tasks):
            column = jnp.sum(
                jnp.where(lane == base + j * experts + e, w, 0.0), axis=1, keepdims=True
            )
            acc[j, rows, :] = acc[j, rows, :] + column * value

    def compute(k, m):
        rows = pl.ds(m * tile, tile)
        weights = buf[k].reshape(-1, wide)
        first[k % 2, rows, :] = jnp.maximum(dot(pooled[rows, :], weights), 0.0).astype(BF16)

        @pl.when(k % 2 == 1)
        def _():
            e = k // 2
            width = dbuf.shape[3]
            low, high = first[0, rows, :], first[1, rows, :]
            total = None
            for h in range(pieces):
                w2 = dbuf[:, e, pl.ds(h * deep_rows, deep_rows), :].reshape(-1, width)
                second = dot(low, w2[:wide]) + dot(high, w2[wide:])
                second = jnp.maximum(second, 0.0).astype(BF16)
                w3 = dbuf[:, e, pl.ds(pieces * deep_rows, dbuf.shape[2] - pieces * deep_rows), :]
                w3 = w3.reshape(-1, width)[h * width : (h + 1) * width]
                part = dot(second, w3)
                total = part if total is None else total + part
            value = jnp.maximum(total, 0.0).astype(BF16)
            outs[e, rows, :] = value
            x_move(e, m).start()
            accumulate(wts, 0, e, m, value)

            @pl.when(e >= 1)
            def _():
                x_move(e - 1, m).wait_recv()
                accumulate(wts_rx, tasks * experts, e - 1, m, outs_rx[e - 1, rows, :])

    @pl.loop(0, chunks + 2)
    def _(i):
        @pl.when(i + 1 < chunks)
        def _():
            own_z(i + 1)

        @pl.when(i >= 2)
        def _():
            sib_wait(i - 2)

        for s in range(max(tiles, nz - 1)):
            if s < tiles:
                @pl.when(i >= 2)
                def _():
                    compute(i - 2, s)
            if s + 1 < nz:
                @pl.when(i < chunks)
                def _():
                    z_step(i, s + 1)

        @pl.when(jnp.logical_and(i >= 1, i <= chunks))
        def _():
            y_step(i - 1)

    for m in range(tiles):
        rows = pl.ds(m * tile, tile)
        x_move(experts - 1, m).wait_recv()
        accumulate(wts_rx, tasks * experts, experts - 1, m, outs_rx[experts - 1, rows, :])
        own, other = wts[rows, :], wts_rx[rows, :]
        lane = lax.broadcasted_iota(jnp.int32, own.shape, 1)
        for j in range(tasks):
            lo = j * experts
            hi = lo + tasks * experts
            mine = jnp.logical_and(lane >= lo, lane < lo + experts)
            theirs = jnp.logical_and(lane >= hi, lane < hi + experts)
            total = jnp.sum(
                jnp.where(mine, own, 0.0) + jnp.where(theirs, other, 0.0), axis=1, keepdims=True
            )
            mix = (acc[j, rows, :] / total).astype(BF16)
            tower = jnp.maximum(dot(mix, tower_hidden[j]), 0.0).astype(BF16).astype(F32)
            out[rows, j : j + 1] = jnp.sum(
                tower * tower_out[j : j + 1, :].astype(F32), axis=1, keepdims=True
            )

    w_move.wait_send()
    for m in range(tiles):
        @pl.loop(0, experts)
        def _(e):
            x_move(e, m).wait_send()

    bmove(b, by.at[0], across).wait_send()

    @pl.loop(0, nz)
    def _(zz):
        for yy in range(2):
            slot = at(zz, yy, c)
            bmove(slot, bsib.at[yy, zz], sib).wait_send()

            @pl.when(jnp.logical_and(z < nz - 1, zz <= z))
            def _():
                bmove(slot, bzp.at[yy, zz], up).wait_send()

            @pl.when(jnp.logical_and(z > 0, zz >= z))
            def _():
                bmove(slot, bzm.at[yy, zz], down).wait_send()

        slot = at(zz, y, c)

        @pl.loop(0, chunks)
        def _(k):
            move(k, slot, sy.at[k, zz], across).wait_send()
            move(k, slot, ssib.at[k, zz], sib).wait_send()
            move(k, slot, ssib.at[k, nz + zz], sib).wait_send()

            @pl.when(jnp.logical_and(z < nz - 1, zz <= z))
            def _():
                move(k, slot, szp.at[k, zz], up).wait_send()

            @pl.when(jnp.logical_and(z > 0, zz >= z))
            def _():
                move(k, slot, szm.at[k, zz], down).wait_send()


def fused(nb, pooled, gate_weight, w_first, w_second, w_third, tower_hidden, tower_out):
    tokens, width_in = pooled.shape
    experts, rows, h1 = w_first.shape
    tasks = tower_hidden.shape[0]
    all_tasks = gate_weight.shape[2]
    deep_rows, deep_width = w_second.shape[1:]
    last_rows, last_width = w_third.shape[1:]
    nz = nb // 4
    chunks, wide = experts * 2, h1 // 2
    tiles = 3 if tokens % (3 * 16) == 0 else 1
    me = lax.axis_index("task")
    gate = jnp.roll(gate_weight, -me * tasks, axis=2)
    gate = jnp.transpose(gate, (0, 2, 1)).reshape(width_in, all_tasks * experts)
    gate = jnp.pad(gate, ((0, 0), (0, 128 - all_tasks * experts)))
    pieces = deep_width // last_width
    packed_rows = pieces * deep_rows + last_rows
    dma = pltpu.SemaphoreType.DMA
    vmem = pl.BlockSpec(memory_space=pltpu.VMEM)
    anywhere = pl.BlockSpec(memory_space=pl.ANY)
    return pl.pallas_call(
        functools.partial(fused_kernel, nb, tiles, deep_rows),
        out_shape=jax.ShapeDtypeStruct((tokens, tasks), F32),
        in_specs=[vmem, vmem, anywhere, anywhere, anywhere, vmem, vmem],
        out_specs=vmem,
        scratch_shapes=[
            pltpu.VMEM((chunks, nb, rows, wide), BF16),
            pltpu.VMEM((nb, experts, packed_rows, last_width), BF16),
            pltpu.VMEM((2, tokens, wide), BF16),
            pltpu.VMEM((experts, tokens, last_width), BF16),
            pltpu.VMEM((experts, tokens, last_width), BF16),
            pltpu.VMEM((tokens, 128), F32),
            pltpu.VMEM((tokens, 128), F32),
            pltpu.VMEM((tasks, tokens, last_width), F32),
            dma((chunks + pieces + 1,)),
            dma((chunks, nb)),
            dma((chunks, nz)),
            dma((chunks, nz)),
            dma((chunks, nz)),
            dma((chunks, 2 * nz)),
            dma((nb,)),
            dma((2, nz)),
            dma((2, nz)),
            dma((1,)),
            dma((2, nz)),
            dma((experts, tiles)),
            dma((experts, tiles)),
            dma((1,)),
            dma((1,)),
        ],
        compiler_params=pltpu.CompilerParams(
            collective_id=0, has_side_effects=True, vmem_limit_bytes=VMEM_BYTES
        ),
    )(pooled, gate, w_first, w_second, w_third, tower_hidden, tower_out)


def gathered_first(pooled, gate_weight, w_first, w_second, w_third, tower_hidden, tower_out):
    tok_rows = pooled.shape[0]
    width_in = pooled.shape[1]
    local_experts = w_first.shape[0]
    all_tasks = gate_weight.shape[2]
    own_tasks = tower_hidden.shape[0]
    gathered = lax.all_gather(w_first, "batch", axis=1, tiled=True)
    deep_rows, deep_width = w_second.shape[1], w_second.shape[2]
    last_rows, last_width = w_third.shape[1], w_third.shape[2]
    halves = deep_width // last_width
    packed = jnp.concatenate(
        [w_second[:, :, i * last_width : (i + 1) * last_width] for i in range(halves)] + [w_third],
        axis=1,
    )
    gathered, packed = lax.optimization_barrier((gathered, packed))
    packed = lax.all_gather(packed, "batch", axis=1, tiled=False)
    second_all = jnp.concatenate(
        [packed[:, :, i * deep_rows : (i + 1) * deep_rows] for i in range(halves)], axis=3
    ).reshape(local_experts, -1, deep_width)
    third_all = packed[:, :, halves * deep_rows :].reshape(local_experts, -1, last_width)
    summed = jnp.einsum("tr,erh->eth", pooled, gathered, preferred_element_type=jnp.float32)
    first = jax.nn.relu(summed).astype(jnp.bfloat16)
    logits = jnp.dot(
        pooled,
        gate_weight.reshape(width_in, local_experts * all_tasks),
        preferred_element_type=jnp.float32,
    )
    weights = jnp.exp(logits.reshape(tok_rows, local_experts, all_tasks))
    gate_total = jnp.sum(weights, axis=1)
    columns = first
    second = jax.nn.relu(
        jnp.einsum(
            "etr,erh->eth",
            columns,
            second_all,
            preferred_element_type=jnp.float32,
        )
    ).astype(jnp.bfloat16)
    columns = second
    expert_out = jax.nn.relu(
        jnp.einsum(
            "etr,erh->eth",
            columns,
            third_all,
            preferred_element_type=jnp.float32,
        )
    ).astype(jnp.bfloat16)
    numer = jnp.einsum("tek,eth->tkh", weights, expert_out.astype(jnp.float32))
    groups = all_tasks // own_tasks
    me = lax.axis_index("task")
    numer_own = lax.dynamic_slice_in_dim(numer, me * own_tasks, own_tasks, 1)
    total_own = lax.dynamic_slice_in_dim(gate_total, me * own_tasks, own_tasks, 1)
    for shift in range(1, groups):
        ring = [(i, (i + shift) % groups) for i in range(groups)]
        other = lax.rem(me + shift, groups) * own_tasks
        numer_sent = lax.dynamic_slice_in_dim(numer, other, own_tasks, 1).astype(jnp.bfloat16)
        total_sent = lax.dynamic_slice_in_dim(gate_total, other, own_tasks, 1)
        numer_own = numer_own + lax.ppermute(numer_sent, "task", ring).astype(jnp.float32)
        total_own = total_own + lax.ppermute(total_sent, "task", ring)
    mix = (numer_own / total_own[:, :, None]).astype(jnp.bfloat16)
    tower = jax.nn.relu(
        jnp.einsum("tkh,khm->tkm", mix, tower_hidden, preferred_element_type=jnp.float32)
    ).astype(jnp.bfloat16)
    return jnp.einsum("tkm,km->tk", tower, tower_out, preferred_element_type=jnp.float32)


def fits(mesh, pooled, gate_weight, w_first, w_second, w_third):
    even = all(w.shape[1] % 16 == 0 for w in (w_first, w_second, w_third))
    lanes = gate_weight.shape[1] * gate_weight.shape[2] <= 128
    return even and lanes and mesh.shape["task"] == 2 and mesh.shape["batch"] % 4 == 0


def solution(mesh):
    placed = (
        P("batch", None),
        P(None, "task", None),
        P("task", "batch", None),
        P("task", "batch", None),
        P("task", "batch", None),
        P("task", None, None),
        P("task", None),
    )

    def per_device(*args):
        if fits(mesh, *args[:5]):
            return fused(mesh.shape["batch"], *args)
        return gathered_first(*args)

    return jax.shard_map(
        per_device, mesh=mesh, in_specs=placed, out_specs=P("batch", "task"), check_vma=False
    )
```

profile of v0, /device:TPU:0, one launch (start us, length us, event | category | flops | bytes accessed | tf_op | source)
XLA Modules:
  0.0 194.6 jit_solution(17409748791912830792)
XLA Ops:
  0.0 1.2 fusion.1
  1.3 0.4 copy.11
  1.7 1.1 pad.4.gate
  2.8 190.0 %shard_map.73 = f32[768,2]{1,0:T(8,128)} custom-call(bf16[768,3328]{1,0:T(8,128)(2,1)} %pooled.1, bf16[3328,128]{1,0:T(8,128)(2,1)} %pad.4.gate, bf16[4,208,1024]{2,1,0:T(8,128)(2,1)} %w_first.1, bf16[4,64,512]{2,1,0:T(8,128)(2,1)} %w_second.1, bf16[4,32,256]{2,1,0:T(8,128)(2,1)} %w_third.1, bf16[2,256,128]{2,1,0:T(8,128)(2,1)} %tower_hidden.1, ...), custom_call_target="tpu_custom_call" | custom-call | tf_op jit(solution)/shard_map/pallas_call | solution.py:346
  192.8 1.7 copy.12
  (2 shorter events, 0.1 us)
where the time goes:
time: 195 us
  Pallas kernels  190 us (97%)
  local copies, waits for them, and re-layouts  3.31 us (2%)
    pallas_call x1, Pallas kernels, fused(): pl.pallas_call(functools.partial(fused_kernel, nb, tiles, deep_rows), out...  190 us

commit v1 on v0

v1 whole, which is shorter than its diff:
```python
import functools

import jax
import jax.numpy as jnp
from jax import lax
from jax.experimental import pallas as pl
from jax.experimental.pallas import tpu as pltpu
from jax.sharding import PartitionSpec as P

MESH = pl.DeviceIdType.MESH
BF16, F32 = jnp.bfloat16, jnp.float32
VMEM_BYTES = 63 * 1024 * 1024
BLOCKS, PIECES = 4, 8


def dot(a, b):
    return jnp.dot(a, b, preferred_element_type=F32)


def fused_kernel(
    nb, pieces,
    pooled, gate, w_first, w_second, w_third, tower_hidden, tower_out, out,
    tok, buf, dbuf, first, out_tx, out_rx, gate_rx, gate_all, wts, acc, th_all, to_all, res, res_rx,
    loc, loc_deep, loc_tok, y_s, y_r, yd_s, yd_r, p_s, p_r, q_s, q_r, g_s, g_r,
    z_r, up_s, dn_s, sib_r, sib_s, o_s, o_r, r_s, r_r,
):
    t, b = lax.axis_index("task"), lax.axis_index("batch")
    nz = nb // 4
    z, y, c = b // 4, (b // 2) % 2, b % 2
    chunks, wide = buf.shape[0], buf.shape[5]
    group = dbuf.shape[3]
    blocks = chunks // group
    tokens = pooled.shape[0]
    half = tokens // 2
    piece = half // pieces
    tasks = tower_hidden.shape[0]
    experts = gate.shape[0]
    deep_rows = w_second.shape[1]
    width = w_third.shape[2]
    splits = w_second.shape[2] // width
    deep = chunks

    def at(zz, yy, cc):
        return zz * 4 + yy * 2 + cc

    across, sib = at(z, 1 - y, c), at(z, y, 1 - c)
    up, down = at(z + 1, y, c), at(z - 1, y, c)

    def remote(src, dst, send, recv, tt, bb):
        return pltpu.make_async_remote_copy(
            src_ref=src, dst_ref=dst, send_sem=send, recv_sem=recv,
            device_id=(tt, bb), device_id_type=MESH,
        )

    def shard(k, yy):
        cols = pl.ds(pl.multiple_of((k % blocks) * wide, 128), wide)
        return w_first.at[yy * group + k // blocks, :, cols]

    def own_copy(k):
        return pltpu.make_async_copy(shard(k, y), buf.at[k, z, y, c], loc.at[k])

    def deep_parts(yy):
        own = pl.ds(yy * group, group)
        to = dbuf.at[z, y, c]
        parts = [
            (w_second.at[own, :, pl.ds(h * width, width)],
             to.at[:, pl.ds(h * deep_rows, deep_rows)])
            for h in range(splits)
        ]
        return parts + [(w_third.at[own], to.at[:, pl.ds(splits * deep_rows, w_third.shape[1])])]

    deep_copies = [
        pltpu.make_async_copy(src, dst, loc_deep.at[n])
        for n, (src, dst) in enumerate(deep_parts(y))
    ]
    deep_across = [
        remote(src, dst, yd_s.at[n], yd_r.at[n], t, across)
        for n, (src, dst) in enumerate(deep_parts(1 - y))
    ]
    tok_copy = pltpu.make_async_copy(pooled, tok.at[pl.ds(0, tokens)], loc_tok.at[0])

    for copy in deep_copies:
        copy.start()

    @pl.loop(0, chunks)
    def _(k):
        own_copy(k).start()

    tok_copy.start()

    barrier = pltpu.get_barrier_semaphore()
    for tt, bb in (
        (t, across), (t, sib), (t, at((z + 1) % nz, y, c)), (t, at((z + nz - 1) % nz, y, c)),
        (1 - t, b), (1 - t, across),
    ):
        pl.semaphore_signal(barrier, inc=1, device_id=(tt, bb), device_id_type=MESH)
    pl.semaphore_wait(barrier, 6)

    def y_move(k):
        return remote(shard(k, 1 - y), buf.at[k, z, y, c], y_s.at[k], y_r.at[k], t, across)

    def tok_rows(h, p):
        return pl.ds(pl.multiple_of(h * half + p * piece, 16), piece)

    def p_move(p):
        rows = pl.ds(pl.multiple_of(tokens + t * half + p * piece, 16), piece)
        return remote(pooled.at[tok_rows(t, p)], tok.at[rows], p_s.at[p], p_r.at[p], t, across)

    def q_move(p):
        rows = pl.ds(pl.multiple_of(tokens + t * half + p * piece, 16), piece)
        return remote(tok.at[rows], tok.at[rows], q_s.at[p], q_r.at[p], 1 - t, b)

    swaps = [
        remote(gate, gate_rx, g_s.at[0], g_r.at[0], 1 - t, b),
        remote(tower_hidden, th_all.at[pl.ds(t * tasks, tasks)], g_s.at[1], g_r.at[1], 1 - t, b),
        remote(tower_out, to_all.at[t], g_s.at[2], g_r.at[2], 1 - t, b),
    ]

    for move in deep_across:
        move.start()
    y_move(0).start()
    y_move(1).start()
    p = 0
    for k in range(2, chunks):
        for _ in range(4 if k == 2 else 2):
            if p < pieces:
                p_move(p).start()
                p += 1
        y_move(k).start()
    for move in swaps:
        move.start()

    def pair(k, zz):
        if k is deep:
            return dbuf.at[zz, :, c]
        return buf.at[k, zz, :, c]

    def slot(k, yy):
        if k is deep:
            return dbuf.at[z, yy, c]
        return buf.at[k, z, yy, c]

    def row(k):
        return chunks if k is deep else k

    def z_own(k, yy, n, what):
        ref = slot(k, yy)

        @pl.when(z < nz - 1)
        def _():
            what(remote(ref, ref, up_s.at[row(k), n], z_r.at[row(k), z], t, up))

        @pl.when(z > 0)
        def _():
            what(remote(ref, ref, dn_s.at[row(k), n], z_r.at[row(k), z], t, down))

    def z_up(k, zz):
        return remote(pair(k, zz), pair(k, zz), up_s.at[row(k), zz], z_r.at[row(k), zz], t, up)

    def z_down(k, zz):
        return remote(pair(k, zz), pair(k, zz), dn_s.at[row(k), zz], z_r.at[row(k), zz], t, down)

    def sib_move(k, zz):
        return remote(pair(k, zz), pair(k, zz), sib_s.at[row(k), zz], sib_r.at[row(k), zz], t, sib)

    def start(copy):
        copy.start()

    def own_start(k):
        if k is deep:
            for copy in deep_copies:
                copy.wait()
        else:
            own_copy(k).wait()
        z_own(k, y, z, start)

    def own_finish(k):
        if k is deep:
            for move in deep_across:
                move.wait_recv()
        else:
            y_move(k).wait_recv()
        z_own(k, 1 - y, nz, start)
        sib_move(k, z).start()

    def z_step(k, d):
        @pl.when(z >= d)
        def _():
            z_up(k, z - d).wait_recv()

            @pl.when(z < nz - 1)
            def _():
                z_up(k, z - d).start()

            sib_move(k, z - d).start()

        @pl.when(z + d < nz)
        def _():
            z_down(k, z + d).wait_recv()

            @pl.when(z > 0)
            def _():
                z_down(k, z + d).start()

            sib_move(k, z + d).start()

    def sib_wait(k):
        @pl.loop(0, nz)
        def _(zz):
            sib_move(k, zz).wait_recv()

    own_start(deep)
    own_start(0)
    own_finish(deep)
    own_finish(0)
    own_start(1)
    own_finish(1)
    for d in range(1, nz):
        z_step(deep, d)

    tok_copy.wait()
    for swap in swaps:
        swap.wait_recv()
    th_all[pl.ds(t * tasks, tasks)] = tower_hidden[...]
    to_all[t] = tower_out[...]
    for e in range(experts):
        n = gate.shape[1]
        gate_all[e * n : (e + 1) * n, :] = gate[e].astype(F32)
        gate_all[(experts + e) * n : (experts + e + 1) * n, :] = gate_rx[e].astype(F32)
    mine = pl.ds(pl.multiple_of(t * half, 16), half)
    wts[...] = jnp.exp(
        lax.dot_general(
            tok[mine, :], gate_all[...].astype(BF16), (((1,), (1,)), ((), ())),
            preferred_element_type=F32,
        )
    )
    acc[...] = jnp.zeros_like(acc)
    sib_wait(deep)

    def route(g):
        near = g // 2
        owner = t + (1 - g % 2) * (1 - 2 * t)
        bb = at(z, jnp.where(near == 1, y, 1 - y), c)
        return near, owner, bb

    def from_slot(owner, i):
        return (jnp.where(owner == t, 0, 1) * 2 + y) * group + i

    def o_move(i, g):
        near, owner, bb = route(g)
        n = from_slot(owner, i)
        return remote(out_tx.at[i, g], out_rx.at[n], o_s.at[i, g], o_r.at[n], owner, bb)

    def compute(k, g):
        near, owner, _ = route(g)
        rows = pl.ds(pl.multiple_of((1 - near) * tokens + owner * half, 16), half)
        cols = pl.ds(pl.multiple_of((k % blocks) * wide, 128), wide)
        weights = buf[k].reshape(-1, wide)
        first[rows, cols] = jnp.maximum(dot(tok[rows, :], weights), 0.0).astype(BF16)

        @pl.when(k % blocks == blocks - 1)
        def _():
            i = k // blocks
            hidden = first[rows, :]
            w3 = dbuf[:, :, :, i, pl.ds(splits * deep_rows, w_third.shape[1]), :].reshape(-1, width)
            total = None
            for h in range(splits):
                w2 = dbuf[:, :, :, i, pl.ds(h * deep_rows, deep_rows), :].reshape(-1, width)
                second = jnp.maximum(dot(hidden, w2), 0.0).astype(BF16)
                part = dot(second, w3[h * width : (h + 1) * width])
                total = part if total is None else total + part
            value = jnp.maximum(total, 0.0).astype(BF16)

            @pl.when(g < 3)
            def _():
                out_tx[i, g] = value
                o_move(i, g).start()

            @pl.when(g == 3)
            def _():
                out_rx[from_slot(t, i)] = value

    def accumulate(far, yy, i):
        value = out_rx[(far * 2 + yy) * group + i].astype(F32)
        n = gate.shape[1]
        for j in range(n):
            col = (far * experts + yy * group + i) * n + j
            acc[j] = acc[j] + wts[:, col : col + 1] * value

    def mix_in(i):
        for far in range(2):
            for yy in range(2):
                n = (far * 2 + yy) * group + i

                def waiting():
                    remote(out_tx.at[i, 0], out_rx.at[n], o_s.at[i, 0], o_r.at[n], t, across).wait_recv()

                if far == 0:
                    pl.when(y != yy)(waiting)
                else:
                    waiting()
                accumulate(far, yy, i)

    def lag(j):
        most = jnp.minimum(j + 1, jnp.maximum(0, 2 * (j - 2)))
        return jnp.where(j == chunks - 1, chunks, most)

    first_lag = 3
    per = -(-pieces // first_lag)

    @pl.loop(0, chunks)
    def _(i):
        @pl.when(i + 2 < chunks)
        def _():
            own_start(i + 2)
            own_finish(i + 2)

        @pl.when(i >= 1)
        def _():
            sib_wait(i - 1)
            compute(i - 1, 2)

        z_step(i, 1)

        @pl.when(i >= 1)
        def _():
            compute(i - 1, 3)

        for d in range(2, nz - 1):
            z_step(i, d)

        @pl.when(i == first_lag + 1)
        def _():
            @pl.loop(0, pieces)
            def _(p):
                q_move(p).wait_recv()

        @pl.when(i > first_lag)
        def _():
            @pl.loop(lag(i - 2), lag(i - 1))
            def _(k):
                compute(k, 0)
                compute(k, 1)

        z_step(i, nz - 1)

        @pl.when(jnp.logical_and(i >= 1, i <= first_lag))
        def _():
            @pl.loop((i - 1) * per, jnp.minimum(i * per, pieces))
            def _(p):
                p_move(p).wait_recv()
                q_move(p).start()

        @pl.when(i == chunks - 1)
        def _():
            for i in range(group - 1):
                mix_in(i)

    last = chunks - 1
    sib_wait(last)

    @pl.loop(lag(last - 1), last)
    def _(k):
        compute(k, 0)
        compute(k, 1)

    @pl.loop(0, 4)
    def _(g):
        compute(last, g)

    mix_in(group - 1)

    n = gate.shape[1]
    for j in range(n):
        total = None
        for e in range(2 * experts):
            w = wts[:, e * n + j : e * n + j + 1]
            total = w if total is None else total + w
        mix = (acc[j] / total).astype(BF16)
        tower = jnp.maximum(dot(mix, th_all[j]), 0.0).astype(BF16)
        vector = jnp.broadcast_to(to_all[j // tasks, j % tasks : j % tasks + 1, :], (16, tower.shape[1]))
        line = lax.dot_general(
            vector, tower, (((1,), (1,)), ((), ())), preferred_element_type=F32
        )
        res[j // tasks, j % tasks : j % tasks + 1, :] = line[:1]
    r_move = remote(res.at[1 - t], res_rx, r_s.at[0], r_r.at[0], 1 - t, b)
    r_move.start()
    out[:, pl.ds(pl.multiple_of(t * half, 128), half)] = res[t, 0:tasks, :]

    for move in deep_across:
        move.wait_send()
    for swap in swaps:
        swap.wait_send()

    @pl.loop(0, pieces)
    def _(p):
        p_move(p).wait_send()
        q_move(p).wait_send()

    for i in range(group):
        @pl.loop(0, 3)
        def _(g):
            o_move(i, g).wait_send()

    def sent(k):
        z_own(k, y, z, lambda copy: copy.wait_send())
        z_own(k, 1 - y, nz, lambda copy: copy.wait_send())

        @pl.loop(0, nz)
        def _(zz):
            sib_move(k, zz).wait_send()

            @pl.when(jnp.logical_and(z < nz - 1, zz < z))
            def _():
                z_up(k, zz).wait_send()

            @pl.when(jnp.logical_and(z > 0, zz > z))
            def _():
                z_down(k, zz).wait_send()

    sent(deep)

    @pl.loop(0, chunks)
    def _(k):
        y_move(k).wait_send()
        sent(k)

    r_move.wait()
    out[:, pl.ds(pl.multiple_of((1 - t) * half, 128), half)] = res_rx[0:tasks, :]


def fused(nb, pooled, gate_weight, w_first, w_second, w_third, tower_hidden, tower_out):
    tokens, width_in = pooled.shape
    experts, rows, h1 = w_first.shape
    tasks = tower_hidden.shape[0]
    all_tasks = gate_weight.shape[2]
    deep_rows, deep_width = w_second.shape[1:]
    last_rows, last_width = w_third.shape[1:]
    nz = nb // 4
    group = experts // 2
    wide = h1 // BLOCKS
    chunks = group * BLOCKS
    half = tokens // 2
    splits = deep_width // last_width
    packed_rows = splits * deep_rows + last_rows
    dma = pltpu.SemaphoreType.DMA
    vmem = pl.BlockSpec(memory_space=pltpu.VMEM)
    anywhere = pl.BlockSpec(memory_space=pl.ANY)
    gate = jnp.transpose(gate_weight, (1, 2, 0))
    lines = pl.pallas_call(
        functools.partial(fused_kernel, nb, PIECES),
        out_shape=jax.ShapeDtypeStruct((tasks, tokens), F32),
        in_specs=[anywhere, vmem, anywhere, anywhere, anywhere, vmem, vmem],
        out_specs=vmem,
        scratch_shapes=[
            pltpu.VMEM((2 * tokens, width_in), BF16),
            pltpu.VMEM((chunks, nz, 2, 2, rows, wide), BF16),
            pltpu.VMEM((nz, 2, 2, group, packed_rows, last_width), BF16),
            pltpu.VMEM((2 * tokens, h1), BF16),
            pltpu.VMEM((group, 3, half, last_width), BF16),
            pltpu.VMEM((4 * group, half, last_width), BF16),
            pltpu.VMEM(gate.shape, BF16),
            pltpu.VMEM((2 * experts * all_tasks, width_in), F32),
            pltpu.VMEM((half, 2 * experts * all_tasks), F32),
            pltpu.VMEM((all_tasks, half, last_width), F32),
            pltpu.VMEM((all_tasks,) + tower_hidden.shape[1:], BF16),
            pltpu.VMEM((2,) + tower_out.shape, BF16),
            pltpu.VMEM((2, 8, half), F32),
            pltpu.VMEM((8, half), F32),
            dma((chunks,)),
            dma((splits + 1,)),
            dma((1,)),
            dma((chunks,)),
            dma((chunks,)),
            dma((splits + 1,)),
            dma((splits + 1,)),
            dma((PIECES,)),
            dma((PIECES,)),
            dma((PIECES,)),
            dma((PIECES,)),
            dma((3,)),
            dma((3,)),
            dma((chunks + 1, nz)),
            dma((chunks + 1, nz + 1)),
            dma((chunks + 1, nz + 1)),
            dma((chunks + 1, nz)),
            dma((chunks + 1, nz)),
            dma((group, 3)),
            dma((4 * group,)),
            dma((1,)),
            dma((1,)),
        ],
        compiler_params=pltpu.CompilerParams(
            collective_id=0, has_side_effects=True, vmem_limit_bytes=VMEM_BYTES
        ),
    )(pooled, gate, w_first, w_second, w_third, tower_hidden, tower_out)
    return lines.T


def gathered_first(pooled, gate_weight, w_first, w_second, w_third, tower_hidden, tower_out):
    tok_rows = pooled.shape[0]
    width_in = pooled.shape[1]
    local_experts = w_first.shape[0]
    all_tasks = gate_weight.shape[2]
    own_tasks = tower_hidden.shape[0]
    gathered = lax.all_gather(w_first, "batch", axis=1, tiled=True)
    deep_rows, deep_width = w_second.shape[1], w_second.shape[2]
    last_rows, last_width = w_third.shape[1], w_third.shape[2]
    halves = deep_width // last_width
    packed = jnp.concatenate(
        [w_second[:, :, i * last_width : (i + 1) * last_width] for i in range(halves)] + [w_third],
        axis=1,
    )
    gathered, packed = lax.optimization_barrier((gathered, packed))
    packed = lax.all_gather(packed, "batch", axis=1, tiled=False)
    second_all = jnp.concatenate(
        [packed[:, :, i * deep_rows : (i + 1) * deep_rows] for i in range(halves)], axis=3
    ).reshape(local_experts, -1, deep_width)
    third_all = packed[:, :, halves * deep_rows :].reshape(local_experts, -1, last_width)
    summed = jnp.einsum("tr,erh->eth", pooled, gathered, preferred_element_type=jnp.float32)
    first = jax.nn.relu(summed).astype(jnp.bfloat16)
    logits = jnp.dot(
        pooled,
        gate_weight.reshape(width_in, local_experts * all_tasks),
        preferred_element_type=jnp.float32,
    )
    weights = jnp.exp(logits.reshape(tok_rows, local_experts, all_tasks))
    gate_total = jnp.sum(weights, axis=1)
    columns = first
    second = jax.nn.relu(
        jnp.einsum(
            "etr,erh->eth",
            columns,
            second_all,
            preferred_element_type=jnp.float32,
        )
    ).astype(jnp.bfloat16)
    columns = second
    expert_out = jax.nn.relu(
        jnp.einsum(
            "etr,erh->eth",
            columns,
            third_all,
            preferred_element_type=jnp.float32,
        )
    ).astype(jnp.bfloat16)
    numer = jnp.einsum("tek,eth->tkh", weights, expert_out.astype(jnp.float32))
    groups = all_tasks // own_tasks
    me = lax.axis_index("task")
    numer_own = lax.dynamic_slice_in_dim(numer, me * own_tasks, own_tasks, 1)
    total_own = lax.dynamic_slice_in_dim(gate_total, me * own_tasks, own_tasks, 1)
    for shift in range(1, groups):
        ring = [(i, (i + shift) % groups) for i in range(groups)]
        other = lax.rem(me + shift, groups) * own_tasks
        numer_sent = lax.dynamic_slice_in_dim(numer, other, own_tasks, 1).astype(jnp.bfloat16)
        total_sent = lax.dynamic_slice_in_dim(gate_total, other, own_tasks, 1)
        numer_own = numer_own + lax.ppermute(numer_sent, "task", ring).astype(jnp.float32)
        total_own = total_own + lax.ppermute(total_sent, "task", ring)
    mix = (numer_own / total_own[:, :, None]).astype(jnp.bfloat16)
    tower = jax.nn.relu(
        jnp.einsum("tkh,khm->tkm", mix, tower_hidden, preferred_element_type=jnp.float32)
    ).astype(jnp.bfloat16)
    return jnp.einsum("tkm,km->tk", tower, tower_out, preferred_element_type=jnp.float32)


def fits(mesh, pooled, gate_weight, w_first, w_second, w_third):
    even = all(w.shape[1] % 16 == 0 for w in (w_first, w_second, w_third))
    tokens, experts = pooled.shape[0], w_first.shape[0]
    cut = tokens % (32 * PIECES) == 0 and tokens % 256 == 0 and experts % 2 == 0
    lanes = w_first.shape[2] % (128 * BLOCKS) == 0 and w_second.shape[2] % w_third.shape[2] == 0
    wanted = (gate_weight.shape[1] * gate_weight.shape[2]) <= 64
    two = mesh.shape["task"] == 2 and gate_weight.shape[2] % 2 == 0
    return even and cut and lanes and wanted and two and mesh.shape["batch"] % 4 == 0


def solution(mesh):
    placed = (
        P("batch", None),
        P(None, "task", None),
        P("task", "batch", None),
        P("task", "batch", None),
        P("task", "batch", None),
        P("task", None, None),
        P("task", None),
    )

    def per_device(*args):
        if fits(mesh, *args[:5]):
            return fused(mesh.shape["batch"], *args)
        return gathered_first(*args)

    return jax.shard_map(
        per_device, mesh=mesh, in_specs=placed, out_specs=P("batch", "task"), check_vma=False
    )
```

time: 195 us -> 185 us (0.949)
  Pallas kernels: 190 us -> 183 us
  local copies, waits for them, and re-layouts: 3.31 us -> 1.29 us
    pallas_call x1, Pallas kernels: 190 us -> 183 us  [fused(): pl.pallas_call(functools.partial(fused_kernel, nb, PIECES), out_shape=jax...]
where the time goes in v1:
time: 185 us; the launch traced here: 184 us
  Pallas kernels  183 us (99%)
    pallas_call x1, Pallas kernels, fused(): pl.pallas_call(functools.partial(fused_kernel, nb, PIECES), out_shape=jax...  183 us

profile of v1, /device:TPU:0, one launch (start us, length us, event | category | flops | bytes accessed | tf_op | source)
XLA Modules:
  0.0 184.4 jit_solution(6042137575878841233)
XLA Ops:
  0.0 183.1 %shard_map.73 = f32[2,768]{1,0:T(2,128)} custom-call(bf16[768,3328]{1,0:T(8,128)(2,1)} %pooled.1, bf16[4,4,3328]{2,1,0:T(4,128)(2,1)} %bitcast.2, bf16[4,208,1024]{2,1,0:T(8,128)(2,1)} %w_first.1, bf16[4,64,512]{2,1,0:T(8,128)(2,1)} %w_second.1, bf16[4,32,256]{2,1,0:T(8,128)(2,1)} %w_third.1, bf16[2,256,128]{2,1,0:T(8,128)(2,1)} %tower_hidden.1, ...), custom_call_target="tpu_custom_call" | custom-call | tf_op jit(solution)/shard_map/pallas_call | solution.py:450
  183.1 1.3 copy.9

commit v2 on v1

--- a/solution.py
+++ b/solution.py
@@ -120,13 +120,10 @@
         move.start()
     y_move(0).start()
     y_move(1).start()
-    p = 0
     for k in range(2, chunks):
-        for _ in range(4 if k == 2 else 2):
-            if p < pieces:
-                p_move(p).start()
-                p += 1
         y_move(k).start()
+    for p in range(pieces):
+        p_move(p).start()
     for move in swaps:
         move.start()
 
@@ -209,12 +206,13 @@
         def _(zz):
             sib_move(k, zz).wait_recv()
 
+    ahead = 3
     own_start(deep)
-    own_start(0)
+    for k in range(ahead):
+        own_start(k)
     own_finish(deep)
-    own_finish(0)
-    own_start(1)
-    own_finish(1)
+    for k in range(ahead):
+        own_finish(k)
     for d in range(1, nz):
         z_step(deep, d)
 
@@ -302,18 +300,19 @@
                 accumulate(far, yy, i)
 
     def lag(j):
-        most = jnp.minimum(j + 1, jnp.maximum(0, 2 * (j - 2)))
-        return jnp.where(j == chunks - 1, chunks, most)
-
-    first_lag = 3
-    per = -(-pieces // first_lag)
+        most = jnp.minimum(j + 1, jnp.maximum(0, 3 * (j - first_lag + 1)))
+        return jnp.where(edge, most, 0)
+
+    first_lag = 4
+    edge = jnp.logical_or(z == 0, z == nz - 1)
+    per = jnp.where(edge, -(-pieces // 3), -(-pieces // first_lag))
 
     @pl.loop(0, chunks)
     def _(i):
-        @pl.when(i + 2 < chunks)
-        def _():
-            own_start(i + 2)
-            own_finish(i + 2)
+        @pl.when(i + ahead < chunks)
+        def _():
+            own_start(i + ahead)
+            own_finish(i + ahead)
 
         @pl.when(i >= 1)
         def _():
@@ -329,7 +328,7 @@
         for d in range(2, nz - 1):
             z_step(i, d)
 
-        @pl.when(i == first_lag + 1)
+        @pl.when(jnp.logical_and(edge, i == first_lag + 1))
         def _():
             @pl.loop(0, pieces)
             def _(p):
@@ -346,29 +345,32 @@
 
         @pl.when(jnp.logical_and(i >= 1, i <= first_lag))
         def _():
-            @pl.loop((i - 1) * per, jnp.minimum(i * per, pieces))
+            @pl.loop(jnp.minimum((i - 1) * per, pieces), jnp.minimum(i * per, pieces))
             def _(p):
                 p_move(p).wait_recv()
                 q_move(p).start()
 
-        @pl.when(i == chunks - 1)
-        def _():
-            for i in range(group - 1):
-                mix_in(i)
-
     last = chunks - 1
-    sib_wait(last)
+
+    @pl.when(jnp.logical_not(edge))
+    def _():
+        @pl.loop(0, pieces)
+        def _(p):
+            q_move(p).wait_recv()
 
     @pl.loop(lag(last - 1), last)
     def _(k):
         compute(k, 0)
         compute(k, 1)
 
+    sib_wait(last)
+
     @pl.loop(0, 4)
     def _(g):
         compute(last, g)
 
-    mix_in(group - 1)
+    for i in range(group):
+        mix_in(i)
 
     n = gate.shape[1]
     for j in range(n):

time: 185 us -> 171 us (0.924)
  Pallas kernels: 183 us -> 170 us
    pallas_call x1, Pallas kernels: 183 us -> 170 us  [fused(): pl.pallas_call(functools.partial(fused_kernel, nb, PIECES), out_shape=jax...]
where the time goes in v2:
time: 171 us
  Pallas kernels  170 us (99%)
    pallas_call x1, Pallas kernels, fused(): pl.pallas_call(functools.partial(fused_kernel, nb, PIECES), out_shape=jax...  170 us

profile of v2, /device:TPU:0, one launch (start us, length us, event | category | flops | bytes accessed | tf_op | source)
XLA Modules:
  0.0 171.0 jit_solution(8857389054036000551)
XLA Ops:
  0.0 169.7 %shard_map.73 = f32[2,768]{1,0:T(2,128)} custom-call(bf16[768,3328]{1,0:T(8,128)(2,1)} %pooled.1, bf16[4,4,3328]{2,1,0:T(4,128)(2,1)} %bitcast.2, bf16[4,208,1024]{2,1,0:T(8,128)(2,1)} %w_first.1, bf16[4,64,512]{2,1,0:T(8,128)(2,1)} %w_second.1, bf16[4,32,256]{2,1,0:T(8,128)(2,1)} %w_third.1, bf16[2,256,128]{2,1,0:T(8,128)(2,1)} %tower_hidden.1, ...), custom_call_target="tpu_custom_call" | custom-call | tf_op jit(solution)/shard_map/pallas_call | solution.py:452
  169.7 1.3 copy.9

commit v3 on v2

v3 whole, which is shorter than its diff:
```python
import functools

import jax
import jax.numpy as jnp
from jax import lax
from jax.experimental import pallas as pl
from jax.experimental.pallas import tpu as pltpu
from jax.sharding import PartitionSpec as P

MESH = pl.DeviceIdType.MESH
BF16, F32 = jnp.bfloat16, jnp.float32
VMEM_BYTES = 63 * 1024 * 1024
BLOCKS, PIECES = 4, 12
SPOTS = (3, 6, 9, 11)
OWN_AHEAD, OWN_AHEAD_EDGE, PAIR_AHEAD, FEED_AHEAD = 5, 3, 4, 1
NEAR_AHEAD, NEAR_AHEAD_EDGE = 3, 3
CROSS_LAG, CROSS_LAG_EDGE, WORK_LAG, WORK_LAG_EDGE = 2, 2, 3, 4
PIECE_LAG, PASS_LAG = 2, 1
FAR_STEPS = (14, 16)


def dot(a, b):
    return jnp.dot(a, b, preferred_element_type=F32)


def fused_kernel(
    nb, pieces,
    pooled, gate, w_first, w_second, w_third, tower_hidden, tower_out, out,
    tok, buf, dbuf, first, out_tx, out_rx, gate_rx, gate_all, wts, acc, th_all, to_all, res, res_rx,
    loc, loc_deep, loc_tok, p_s, p_r, q_s, q_r, g_s, g_r,
    got, z_s, y_s, f_s, sib_r, sib_s, o_s, o_r, far_s, far_r, r_s, r_r,
):
    t, b = lax.axis_index("task"), lax.axis_index("batch")
    nz = nb // 4
    z, y, c = b // 4, (b // 2) % 2, b % 2
    high = z // (nz // 2)
    edge = jnp.logical_or(z == 0, z == nz - 1)
    inner = jnp.logical_not(edge)
    zp = jnp.where(edge, z + 1 - 2 * high, z - 1 + 2 * high)
    zm = nz - 1 - z
    zq = nz - 1 - zp
    chunks, wide = buf.shape[0], buf.shape[5]
    experts = dbuf.shape[0]
    blocks = chunks // experts
    tokens = pooled.shape[0]
    half = tokens // 2
    piece = half // pieces
    tasks = tower_hidden.shape[0]
    deep_rows = w_second.shape[1]
    width = w_third.shape[2]
    splits = w_second.shape[2] // width

    def at(zz, yy, cc):
        return zz * 4 + yy * 2 + cc

    across, sib = at(z, 1 - y, c), at(z, y, 1 - c)

    def both(p, q):
        return jnp.logical_and(p, q)

    def either(p, q):
        return jnp.logical_or(p, q)

    def remote(src, dst, send, recv, tt, bb):
        return pltpu.make_async_remote_copy(
            src_ref=src, dst_ref=dst, send_sem=send, recv_sem=recv,
            device_id=(tt, bb), device_id_type=MESH,
        )

    def passed(n):
        count = 0
        for spot in SPOTS:
            count = count + jnp.where(n > spot, 1, 0)
        return count

    def zeroth(n):
        hit = n == SPOTS[0]
        for spot in SPOTS[1:]:
            hit = either(hit, n == spot)
        return hit

    def rank(n):
        return n - passed(n)

    def expert(n):
        return jnp.where(zeroth(n), 0, 1 + rank(n) // blocks)

    def block(n):
        return jnp.where(zeroth(n), passed(n), rank(n) % blocks)

    def own_copy(n):
        cols = pl.ds(pl.multiple_of(block(n) * wide, 128), wide)
        return pltpu.make_async_copy(
            w_first.at[expert(n), :, cols], buf.at[n, z, y, c], loc.at[n]
        )

    deep_copies = [
        pltpu.make_async_copy(
            w_second.at[:, :, pl.ds(h * width, width)],
            dbuf.at[:, z, y, c, pl.ds(h * deep_rows, deep_rows)], loc_deep.at[h],
        )
        for h in range(splits)
    ] + [
        pltpu.make_async_copy(
            w_third, dbuf.at[:, z, y, c, pl.ds(splits * deep_rows, w_third.shape[1])],
            loc_deep.at[splits],
        )
    ]
    tok_copy = pltpu.make_async_copy(pooled, tok.at[pl.ds(0, tokens)], loc_tok.at[0])

    for copy in deep_copies:
        copy.start()

    @pl.loop(0, chunks)
    def _(n):
        own_copy(n).start()

    tok_copy.start()

    barrier = pltpu.get_barrier_semaphore()
    for tt, bb in (
        (t, across), (t, sib), (t, at(zp, y, c)), (t, at(zm, y, c)), (1 - t, b),
        (1 - t, at(zp, y, c)),
    ):
        pl.semaphore_signal(barrier, inc=1, device_id=(tt, bb), device_id_type=MESH)
    pl.semaphore_wait(barrier, 6)

    swaps = [
        remote(gate, gate_rx, g_s.at[0], g_r.at[0], 1 - t, b),
        remote(tower_hidden, th_all.at[pl.ds(t * tasks, tasks)], g_s.at[1], g_r.at[1], 1 - t, b),
        remote(tower_out, to_all.at[t], g_s.at[2], g_r.at[2], 1 - t, b),
    ]
    for move in swaps:
        move.start()

    def chunk(n):
        return (lambda zz, yy: buf.at[n, zz, yy, c], lambda zz: buf.at[n, zz, :, c],
                n, zeroth(n), jnp.logical_not(zeroth(n)))

    def deep(e):
        return (lambda zz, yy: dbuf.at[e, zz, yy, c], lambda zz: dbuf.at[e, zz, :, c],
                chunks + e, e >= 0, e != 0)

    def hop(it, zz, yy, sem, bb):
        ref = it[0](zz, yy)
        return remote(ref, ref, sem, got.at[it[2], zz, yy], t, bb)

    def to_mid(it, zz, yy, key):
        return hop(it, zz, yy, z_s.at[it[2], key], at(zm, y, c))

    def to_pair(it, zz, yy, key):
        return hop(it, zz, yy, f_s.at[it[2], key], at(zp, y, c))

    def to_side(it, zz):
        return hop(it, zz, y, y_s.at[it[2], zz], across)

    def to_sib(it, zz):
        ref = it[1](zz)
        return remote(ref, ref, sib_s.at[it[2], zz], sib_r.at[it[2], zz], t, sib)

    def landed(it, zz, yy):
        to_pair(it, zz, yy, 0).wait_recv()

    def own(it):
        _, _, _, dup, ends = it
        to_side(it, z).start()

        @pl.when(inner)
        def _():
            to_mid(it, z, y, 0).start()

        @pl.when(either(edge, ends))
        def _():
            to_pair(it, z, y, 0).start()

    def finish(it):
        _, _, _, dup, ends = it
        landed(it, z, 1 - y)

        @pl.when(both(dup, inner))
        def _():
            to_mid(it, z, 1 - y, 1).start()

        @pl.when(both(dup, either(edge, ends)))
        def _():
            to_pair(it, z, 1 - y, 1).start()

        @pl.when(either(inner, ends))
        def _():
            to_sib(it, z).start()

    def feed(it):
        _, _, _, dup, ends = it
        landed(it, zp, y)
        to_mid(it, zp, y, 2).start()

        @pl.when(dup)
        def _():
            landed(it, zp, 1 - y)
            to_mid(it, zp, 1 - y, 3).start()
            to_sib(it, zp).start()

        @pl.when(jnp.logical_not(dup))
        def _():
            to_side(it, zp).start()

    def take(it, key, zz):
        _, _, _, dup, ends = it
        landed(it, zz, y)

        @pl.when(both(inner, ends))
        def _():
            to_pair(it, zz, y, key).start()

        @pl.when(dup)
        def _():
            landed(it, zz, 1 - y)

            @pl.when(both(inner, ends))
            def _():
                to_pair(it, zz, 1 - y, key + 1).start()

            to_sib(it, zz).start()

        @pl.when(jnp.logical_not(dup))
        def _():
            to_side(it, zz).start()

    def near(it):
        @pl.when(either(inner, it[4]))
        def _():
            take(it, 2, jnp.where(inner, zm, zp))

    def far(it):
        @pl.when(either(inner, it[4]))
        def _():
            take(it, 4, zq)

        @pl.when(both(edge, it[4]))
        def _():
            take(it, 2, zm)

    def cross(it):
        @pl.when(jnp.logical_not(it[3]))
        def _():
            for zz in (zp, zm, zq):
                landed(it, zz, 1 - y)
                to_sib(it, zz).start()

    def sib_wait(it):
        @pl.loop(0, nz)
        def _(zz):
            to_sib(it, zz).wait_recv()

    def stage(n, step):
        @pl.when(block(n) == 2)
        def _():
            step(deep(expert(n)))

        step(chunk(n))

    def own_at(n):
        own_copy(n).wait()
        stage(n, own)

    def tok_rows(h, p):
        return pl.ds(pl.multiple_of(h * half + p * piece, 16), piece)

    def far_rows(p):
        return pl.ds(pl.multiple_of(tokens + t * half + p * piece, 16), piece)

    def p_move(p):
        return remote(
            pooled.at[tok_rows(t, p)], tok.at[far_rows(p)], p_s.at[p], p_r.at[p], t, at(zp, y, c)
        )

    def q_move(p):
        rows = far_rows(p)
        return remote(tok.at[rows], tok.at[rows], q_s.at[p], q_r.at[p], 1 - t, b)

    for copy in deep_copies:
        copy.wait()
    own_ahead = jnp.where(edge, OWN_AHEAD_EDGE, OWN_AHEAD)

    @pl.loop(0, own_ahead)
    def _(n):
        own_at(n)

    @pl.when(edge)
    def _():
        @pl.loop(0, chunks)
        def _(n):
            @pl.when(n + OWN_AHEAD_EDGE < chunks)
            def _():
                own_at(n + OWN_AHEAD_EDGE)

            stage(n, finish)

            @pl.when(both(n > PIECE_LAG, n <= PIECE_LAG + pieces))
            def _():
                p_move(n - PIECE_LAG - 1).start()

    @pl.when(inner)
    def _():
        @pl.loop(0, PAIR_AHEAD)
        def _(n):
            stage(n, finish)

        @pl.loop(0, FEED_AHEAD)
        def _(n):
            stage(n, feed)

    tok_copy.wait()
    for swap in swaps:
        swap.wait_recv()
    th_all[pl.ds(t * tasks, tasks)] = tower_hidden[...]
    to_all[t] = tower_out[...]
    every = gate.shape[1]
    for e in range(experts):
        gate_all[e * every : (e + 1) * every, :] = gate[e].astype(F32)
        gate_all[(experts + e) * every : (experts + e + 1) * every, :] = gate_rx[e].astype(F32)
    mine = pl.ds(pl.multiple_of(t * half, 16), half)
    raw = jnp.exp(
        lax.dot_general(
            tok[mine, :], gate_all[...].astype(BF16), (((1,), (1,)), ((), ())),
            preferred_element_type=F32,
        )
    )
    lane = lax.broadcasted_iota(jnp.int32, raw.shape, 1)
    below = jnp.ones_like(raw)
    for j in range(every):
        own_task = lane % every == j
        total = jnp.sum(jnp.where(own_task, raw, 0.0), axis=1, keepdims=True)
        below = jnp.where(own_task, total, below)
    wts[...] = raw / below
    acc[...] = jnp.zeros_like(acc)

    def o_move(e):
        slot = experts + e
        return remote(out_tx.at[e], out_rx.at[slot], o_s.at[e], o_r.at[slot], 1 - t, b)

    def narrow(e, hidden):
        w3 = dbuf[e, :, :, :, pl.ds(splits * deep_rows, w_third.shape[1]), :].reshape(-1, width)
        total = None
        for h in range(splits):
            w2 = dbuf[e, :, :, :, pl.ds(h * deep_rows, deep_rows), :].reshape(-1, width)
            second = jnp.maximum(dot(hidden, w2), 0.0).astype(BF16)
            part = dot(second, w3[h * width : (h + 1) * width])
            total = part if total is None else total + part
        return jnp.maximum(total, 0.0).astype(BF16)

    def widen(n, rows, kept):
        cols = pl.ds(pl.multiple_of(block(n) * wide, 128), wide)
        weights = buf[n].reshape(-1, wide)
        first[kept, cols] = jnp.maximum(dot(tok[rows, :], weights), 0.0).astype(BF16)

    def compute(n, g):
        owner = 1 - t if g == 0 else t
        base = jnp.where(zeroth(n), 0, 2 * tokens)
        rows = pl.ds(pl.multiple_of(owner * half, 16), half)
        kept = pl.ds(pl.multiple_of(base + owner * half, 16), half)
        widen(n, rows, kept)

        @pl.when(block(n) == blocks - 1)
        def _():
            e = expert(n)
            value = narrow(e, first[kept, :])
            if g == 0:
                out_tx[e] = value
                o_move(e).start()
            else:
                out_rx[e] = value

    part = half // 2

    def far_move(f, side):
        owner = t + (1 - side) * (1 - 2 * t)
        rows = pl.ds(pl.multiple_of(f * part, 16), part)
        return remote(
            out_tx.at[experts + side, rows], out_rx.at[(1 - side) * experts, rows],
            far_s.at[side, f], far_r.at[1 - side, f], owner, at(zp, y, c),
        )

    def compute_far(f, side):
        owner = t + (1 - side) * (1 - 2 * t)
        rows = pl.ds(pl.multiple_of(tokens + owner * half + f * part, 16), part)

        @pl.loop(0, blocks)
        def _(s):
            spot = SPOTS[0]
            for k in range(1, blocks):
                spot = jnp.where(s == k, SPOTS[k], spot)
            widen(spot, rows, rows)

        there = pl.ds(pl.multiple_of(f * part, 16), part)
        out_tx[experts + side, there, :] = narrow(0, first[rows, :])
        far_move(f, side).start()

    near_ahead = jnp.where(edge, NEAR_AHEAD_EDGE, NEAR_AHEAD)

    @pl.loop(0, near_ahead)
    def _(n):
        stage(n, near)

    cross_lag = jnp.where(edge, CROSS_LAG_EDGE, CROSS_LAG)
    work_lag = jnp.where(edge, WORK_LAG_EDGE, WORK_LAG)

    @pl.loop(0, chunks + max(WORK_LAG, WORK_LAG_EDGE))
    def _(i):
        @pl.when(inner)
        def _():
            @pl.when(i + OWN_AHEAD < chunks)
            def _():
                own_at(i + OWN_AHEAD)

            @pl.when(i + PAIR_AHEAD < chunks)
            def _():
                stage(i + PAIR_AHEAD, finish)

            @pl.when(i + FEED_AHEAD < chunks)
            def _():
                stage(i + FEED_AHEAD, feed)

        n = i - work_lag
        ready = both(both(n >= 0, n < chunks), either(inner, jnp.logical_not(zeroth(n))))

        @pl.when(ready)
        def _():
            stage(n, sib_wait)
            compute(n, 0)

        @pl.when(i + near_ahead < chunks)
        def _():
            stage(i + near_ahead, near)

        @pl.when(i < chunks)
        def _():
            stage(i, far)

        @pl.when(ready)
        def _():
            compute(n, 1)

        k = i - cross_lag

        @pl.when(both(k >= 0, k < chunks))
        def _():
            stage(k, cross)

        @pl.when(both(inner, both(i > PASS_LAG, i <= PASS_LAG + pieces)))
        def _():
            p_move(i - PASS_LAG - 1).wait_recv()
            q_move(i - PASS_LAG - 1).start()

        for f in range(2):
            @pl.when(both(inner, i == FAR_STEPS[f]))
            def _():
                @pl.loop(f * pieces // 2, (f + 1) * pieces // 2)
                def _(p):
                    q_move(p).wait_recv()

        first_far = both(i >= FAR_STEPS[0], i < FAR_STEPS[0] + 2)
        second_far = both(i >= FAR_STEPS[1], i < FAR_STEPS[1] + 2)

        @pl.when(both(inner, either(first_far, second_far)))
        def _():
            f = jnp.where(i >= FAR_STEPS[1], 1, 0)
            compute_far(f, i - jnp.where(f == 1, FAR_STEPS[1], FAR_STEPS[0]))

    def accumulate(far, e):
        value = out_rx[far * experts + e].astype(F32)
        for j in range(every):
            col = (far * experts + e) * every + j
            acc[j] = acc[j] + wts[:, col : col + 1] * value

    def waiting(e):
        o_move(e).wait_recv()

    def waiting_far(far):
        for f in range(2):
            far_move(f, 1 - far).wait_recv()

    for e in range(1, experts):
        accumulate(0, e)
    for e in range(1, experts - 1):
        waiting(e)
        accumulate(1, e)
    pl.when(edge)(lambda: waiting_far(0))
    accumulate(0, 0)
    pl.when(edge)(lambda: waiting_far(1))
    pl.when(inner)(lambda: waiting(0))
    accumulate(1, 0)
    for swap in swaps:
        swap.wait_send()

    @pl.when(edge)
    def _():
        @pl.loop(0, pieces)
        def _(p):
            p_move(p).wait_send()

    @pl.when(inner)
    def _():
        @pl.loop(0, pieces)
        def _(p):
            q_move(p).wait_send()

        o_move(0).wait_send()
        for f in range(2):
            for side in range(2):
                far_move(f, side).wait_send()

    @pl.loop(1, experts)
    def _(e):
        o_move(e).wait_send()

    def sent(it):
        _, _, _, dup, ends = it
        to_side(it, z).wait_send()

        @pl.when(inner)
        def _():
            to_mid(it, z, y, 0).wait_send()
            to_mid(it, zp, y, 2).wait_send()

            @pl.when(dup)
            def _():
                to_mid(it, z, 1 - y, 1).wait_send()
                to_mid(it, zp, 1 - y, 3).wait_send()

            @pl.when(ends)
            def _():
                to_pair(it, zm, y, 2).wait_send()
                to_pair(it, zq, y, 4).wait_send()

                @pl.when(dup)
                def _():
                    to_pair(it, zm, 1 - y, 3).wait_send()
                    to_pair(it, zq, 1 - y, 5).wait_send()

        @pl.when(either(edge, ends))
        def _():
            to_pair(it, z, y, 0).wait_send()

            @pl.when(dup)
            def _():
                to_pair(it, z, 1 - y, 1).wait_send()

        @pl.when(jnp.logical_not(dup))
        def _():
            for zz in (zp, zm, zq):
                to_side(it, zz).wait_send()

        @pl.when(either(inner, ends))
        def _():
            @pl.loop(0, nz)
            def _(zz):
                to_sib(it, zz).wait_send()

    @pl.loop(0, chunks)
    def _(n):
        sent(chunk(n))

    @pl.loop(0, experts)
    def _(e):
        sent(deep(e))

    waiting(experts - 1)
    accumulate(1, experts - 1)

    for j in range(every):
        mix = acc[j].astype(BF16)
        tower = jnp.maximum(dot(mix, th_all[j]), 0.0).astype(BF16)
        vector = jnp.broadcast_to(to_all[j // tasks, j % tasks : j % tasks + 1, :], (16, tower.shape[1]))
        line = lax.dot_general(
            vector, tower, (((1,), (1,)), ((), ())), preferred_element_type=F32
        )
        res[j // tasks, j % tasks : j % tasks + 1, :] = line[:1]
    r_move = remote(res.at[1 - t], res_rx, r_s.at[0], r_r.at[0], 1 - t, b)
    r_move.start()
    out[:, pl.ds(pl.multiple_of(t * half, 128), half)] = res[t, 0:tasks, :]

    r_move.wait()
    out[:, pl.ds(pl.multiple_of((1 - t) * half, 128), half)] = res_rx[0:tasks, :]


def fused(nb, pooled, gate_weight, w_first, w_second, w_third, tower_hidden, tower_out):
    tokens, width_in = pooled.shape
    experts, rows, h1 = w_first.shape
    tasks = tower_hidden.shape[0]
    all_tasks = gate_weight.shape[2]
    deep_rows, deep_width = w_second.shape[1:]
    last_rows, last_width = w_third.shape[1:]
    nz = nb // 4
    wide = h1 // BLOCKS
    chunks = experts * BLOCKS
    items = chunks + experts
    half = tokens // 2
    splits = deep_width // last_width
    packed_rows = splits * deep_rows + last_rows
    dma = pltpu.SemaphoreType.DMA
    vmem = pl.BlockSpec(memory_space=pltpu.VMEM)
    anywhere = pl.BlockSpec(memory_space=pl.ANY)
    gate = jnp.transpose(gate_weight, (1, 2, 0))
    lines = pl.pallas_call(
        functools.partial(fused_kernel, nb, PIECES),
        out_shape=jax.ShapeDtypeStruct((tasks, tokens), F32),
        in_specs=[anywhere, vmem, anywhere, anywhere, anywhere, vmem, vmem],
        out_specs=vmem,
        scratch_shapes=[
            pltpu.VMEM((2 * tokens, width_in), BF16),
            pltpu.VMEM((chunks, nz, 2, 2, rows, wide), BF16),
            pltpu.VMEM((experts, nz, 2, 2, packed_rows, last_width), BF16),
            pltpu.VMEM((3 * tokens, h1), BF16),
            pltpu.VMEM((experts + 2, half, last_width), BF16),
            pltpu.VMEM((2 * experts, half, last_width), BF16),
            pltpu.VMEM(gate.shape, BF16),
            pltpu.VMEM((2 * experts * all_tasks, width_in), F32),
            pltpu.VMEM((half, 2 * experts * all_tasks), F32),
            pltpu.VMEM((all_tasks, half, last_width), F32),
            pltpu.VMEM((all_tasks,) + tower_hidden.shape[1:], BF16),
            pltpu.VMEM((2,) + tower_out.shape, BF16),
            pltpu.VMEM((2, 8, half), F32),
            pltpu.VMEM((8, half), F32),
            dma((chunks,)),
            dma((splits + 1,)),
            dma((1,)),
            dma((PIECES,)),
            dma((PIECES,)),
            dma((PIECES,)),
            dma((PIECES,)),
            dma((3,)),
            dma((3,)),
            dma((items, nz, 2)),
            dma((items, 4)),
            dma((items, nz)),
            dma((items, 6)),
            dma((items, nz)),
            dma((items, nz)),
            dma((experts,)),
            dma((2 * experts,)),
            dma((2, 2)),
            dma((2, 2)),
            dma((1,)),
            dma((1,)),
        ],
        compiler_params=pltpu.CompilerParams(
            collective_id=0, has_side_effects=True, vmem_limit_bytes=VMEM_BYTES
        ),
    )(pooled, gate, w_first, w_second, w_third, tower_hidden, tower_out)
    return lines.T


def gathered_first(pooled, gate_weight, w_first, w_second, w_third, tower_hidden, tower_out):
    tok_rows = pooled.shape[0]
    width_in = pooled.shape[1]
    local_experts = w_first.shape[0]
    all_tasks = gate_weight.shape[2]
    own_tasks = tower_hidden.shape[0]
    gathered = lax.all_gather(w_first, "batch", axis=1, tiled=True)
    deep_rows, deep_width = w_second.shape[1], w_second.shape[2]
    last_rows, last_width = w_third.shape[1], w_third.shape[2]
    halves = deep_width // last_width
    packed = jnp.concatenate(
        [w_second[:, :, i * last_width : (i + 1) * last_width] for i in range(halves)] + [w_third],
        axis=1,
    )
    gathered, packed = lax.optimization_barrier((gathered, packed))
    packed = lax.all_gather(packed, "batch", axis=1, tiled=False)
    second_all = jnp.concatenate(
        [packed[:, :, i * deep_rows : (i + 1) * deep_rows] for i in range(halves)], axis=3
    ).reshape(local_experts, -1, deep_width)
    third_all = packed[:, :, halves * deep_rows :].reshape(local_experts, -1, last_width)
    summed = jnp.einsum("tr,erh->eth", pooled, gathered, preferred_element_type=jnp.float32)
    first = jax.nn.relu(summed).astype(jnp.bfloat16)
    logits = jnp.dot(
        pooled,
        gate_weight.reshape(width_in, local_experts * all_tasks),
        preferred_element_type=jnp.float32,
    )
    weights = jnp.exp(logits.reshape(tok_rows, local_experts, all_tasks))
    gate_total = jnp.sum(weights, axis=1)
    columns = first
    second = jax.nn.relu(
        jnp.einsum(
            "etr,erh->eth",
            columns,
            second_all,
            preferred_element_type=jnp.float32,
        )
    ).astype(jnp.bfloat16)
    columns = second
    expert_out = jax.nn.relu(
        jnp.einsum(
            "etr,erh->eth",
            columns,
            third_all,
            preferred_element_type=jnp.float32,
        )
    ).astype(jnp.bfloat16)
    numer = jnp.einsum("tek,eth->tkh", weights, expert_out.astype(jnp.float32))
    groups = all_tasks // own_tasks
    me = lax.axis_index("task")
    numer_own = lax.dynamic_slice_in_dim(numer, me * own_tasks, own_tasks, 1)
    total_own = lax.dynamic_slice_in_dim(gate_total, me * own_tasks, own_tasks, 1)
    for shift in range(1, groups):
        ring = [(i, (i + shift) % groups) for i in range(groups)]
        other = lax.rem(me + shift, groups) * own_tasks
        numer_sent = lax.dynamic_slice_in_dim(numer, other, own_tasks, 1).astype(jnp.bfloat16)
        total_sent = lax.dynamic_slice_in_dim(gate_total, other, own_tasks, 1)
        numer_own = numer_own + lax.ppermute(numer_sent, "task", ring).astype(jnp.float32)
        total_own = total_own + lax.ppermute(total_sent, "task", ring)
    mix = (numer_own / total_own[:, :, None]).astype(jnp.bfloat16)
    tower = jax.nn.relu(
        jnp.einsum("tkh,khm->tkm", mix, tower_hidden, preferred_element_type=jnp.float32)
    ).astype(jnp.bfloat16)
    return jnp.einsum("tkm,km->tk", tower, tower_out, preferred_element_type=jnp.float32)


def fits(mesh, pooled, gate_weight, w_first, w_second, w_third):
    even = all(w.shape[1] % 16 == 0 for w in (w_first, w_second, w_third))
    tokens, experts = pooled.shape[0], w_first.shape[0]
    cut = tokens % (32 * PIECES) == 0 and tokens % 256 == 0 and experts >= 4
    lanes = w_first.shape[2] % (128 * BLOCKS) == 0 and w_second.shape[2] % w_third.shape[2] == 0
    wanted = (gate_weight.shape[1] * gate_weight.shape[2]) <= 64
    two = mesh.shape["task"] == 2 and gate_weight.shape[2] % 2 == 0
    held = (experts * (w_first.shape[1] * w_first.shape[2]) + tokens * pooled.shape[1] // 8) * 32
    return even and cut and lanes and wanted and two and mesh.shape["batch"] == 16 and held < 2**26


def solution(mesh):
    placed = (
        P("batch", None),
        P(None, "task", None),
        P("task", "batch", None),
        P("task", "batch", None),
        P("task", "batch", None),
        P("task", None, None),
        P("task", None),
    )

    def per_device(*args):
        if fits(mesh, *args[:5]):
            return fused(mesh.shape["batch"], *args)
        return gathered_first(*args)

    return jax.shard_map(
        per_device, mesh=mesh, in_specs=placed, out_specs=P("batch", "task"), check_vma=False
    )
```

time: 171 us -> 165 us (0.965)
  Pallas kernels: 170 us -> 164 us
    pallas_call x1, Pallas kernels: 170 us -> 164 us  [fused(): pl.pallas_call(functools.partial(fused_kernel, nb, PIECES), out_shape=jax...]
where the time goes in v3:
time: 165 us
  Pallas kernels  164 us (99%)
    pallas_call x1, Pallas kernels, fused(): pl.pallas_call(functools.partial(fused_kernel, nb, PIECES), out_shape=jax...  164 us

profile of v3, /device:TPU:0, one launch (start us, length us, event | category | flops | bytes accessed | tf_op | source)
XLA Modules:
  0.0 164.9 jit_solution(18248999578896034200)
XLA Ops:
  0.0 163.6 %shard_map.73 = f32[2,768]{1,0:T(2,128)} custom-call(bf16[768,3328]{1,0:T(8,128)(2,1)} %pooled.1, bf16[4,4,3328]{2,1,0:T(4,128)(2,1)} %bitcast.2, bf16[4,208,1024]{2,1,0:T(8,128)(2,1)} %w_first.1, bf16[4,64,512]{2,1,0:T(8,128)(2,1)} %w_second.1, bf16[4,32,256]{2,1,0:T(8,128)(2,1)} %w_third.1, bf16[2,256,128]{2,1,0:T(8,128)(2,1)} %tower_hidden.1, ...), custom_call_target="tpu_custom_call" | custom-call | tf_op jit(solution)/shard_map/pallas_call | solution.py:605
  163.6 1.3 copy.9

commit v4 on v3

--- a/solution.py
+++ b/solution.py
@@ -311,29 +311,7 @@
             stage(n, feed)
 
     tok_copy.wait()
-    for swap in swaps:
-        swap.wait_recv()
-    th_all[pl.ds(t * tasks, tasks)] = tower_hidden[...]
-    to_all[t] = tower_out[...]
     every = gate.shape[1]
-    for e in range(experts):
-        gate_all[e * every : (e + 1) * every, :] = gate[e].astype(F32)
-        gate_all[(experts + e) * every : (experts + e + 1) * every, :] = gate_rx[e].astype(F32)
-    mine = pl.ds(pl.multiple_of(t * half, 16), half)
-    raw = jnp.exp(
-        lax.dot_general(
-            tok[mine, :], gate_all[...].astype(BF16), (((1,), (1,)), ((), ())),
-            preferred_element_type=F32,
-        )
-    )
-    lane = lax.broadcasted_iota(jnp.int32, raw.shape, 1)
-    below = jnp.ones_like(raw)
-    for j in range(every):
-        own_task = lane % every == j
-        total = jnp.sum(jnp.where(own_task, raw, 0.0), axis=1, keepdims=True)
-        below = jnp.where(own_task, total, below)
-    wts[...] = raw / below
-    acc[...] = jnp.zeros_like(acc)
 
     def o_move(e):
         slot = experts + e
@@ -432,6 +410,31 @@
         @pl.when(i + near_ahead < chunks)
         def _():
             stage(i + near_ahead, near)
+
+        @pl.when(i == 1)
+        def _():
+            for swap in swaps:
+                swap.wait_recv()
+            th_all[pl.ds(t * tasks, tasks)] = tower_hidden[...]
+            to_all[t] = tower_out[...]
+            for e in range(experts):
+                gate_all[e * every : (e + 1) * every, :] = gate[e].astype(F32)
+                gate_all[(experts + e) * every : (experts + e + 1) * every, :] = gate_rx[e].astype(F32)
+            mine = pl.ds(pl.multiple_of(t * half, 16), half)
+            raw = jnp.exp(
+                lax.dot_general(
+                    tok[mine, :], gate_all[...].astype(BF16), (((1,), (1,)), ((), ())),
+                    preferred_element_type=F32,
+                )
+            )
+            lane = lax.broadcasted_iota(jnp.int32, raw.shape, 1)
+            below = jnp.ones_like(raw)
+            for j in range(every):
+                own_task = lane % every == j
+                total = jnp.sum(jnp.where(own_task, raw, 0.0), axis=1, keepdims=True)
+                below = jnp.where(own_task, total, below)
+            wts[...] = raw / below
+            acc[...] = jnp.zeros_like(acc)
 
         @pl.when(i < chunks)
         def _():

time: 165 us -> 165 us (level)
  no operation moved by 1% of the time
where the time goes in v4:
time: 165 us
  Pallas kernels  164 us (99%)
    pallas_call x1, Pallas kernels, fused(): pl.pallas_call(functools.partial(fused_kernel, nb, PIECES), out_shape=jax...  164 us

profile of v4, /device:TPU:0, one launch (start us, length us, event | category | flops | bytes accessed | tf_op | source)
XLA Modules:
  0.0 164.9 jit_solution(15279166475095927691)
XLA Ops:
  0.0 163.6 %shard_map.73 = f32[2,768]{1,0:T(2,128)} custom-call(bf16[768,3328]{1,0:T(8,128)(2,1)} %pooled.1, bf16[4,4,3328]{2,1,0:T(4,128)(2,1)} %bitcast.2, bf16[4,208,1024]{2,1,0:T(8,128)(2,1)} %w_first.1, bf16[4,64,512]{2,1,0:T(8,128)(2,1)} %w_second.1, bf16[4,32,256]{2,1,0:T(8,128)(2,1)} %w_third.1, bf16[2,256,128]{2,1,0:T(8,128)(2,1)} %tower_hidden.1, ...), custom_call_target="tpu_custom_call" | custom-call | tf_op jit(solution)/shard_map/pallas_call | solution.py:608
  163.6 1.3 copy.9
